TPU v7x, 128 devices: a whole 4x4x4 slice. The times are simulated.
128 devices in a mesh: gx: 16 (over x_lo, z, core), gy: 8 (over y, x_hi).
Axes of the slice: x: 4 (x_hi: 2, x_lo: 2; x = x_hi * 2 + x_lo), y: 4, z: 4, core: 2. Of those that a mesh axis runs over, the one named last changes fastest.
Arguments:
- right_side: float32 [256, 256, 128], P('gx', 'gy'), may hold values from -6 to 6
- shift: float32 [256, 256, 128], P('gx', 'gy'), may hold values from 0.5 to 8
Outputs:
- solution_field: float32 [256, 256, 128], P('gx', 'gy')
- residual: float32 [256, 256, 128], P('gx', 'gy')
All inputs are finite; a program needn't handle non-finite values.
Results may differ from a plain program's by a relative error of at most 0.0003.
Values sent between devices are 32-bit elements; how exact they have to be, the bound alone decides.
No kernel may reach another device: no remote copies, remote signals or barrier semaphores. Data moves between devices by JAX's collectives and lax.ppermute only.
A program may use at most 128 MiB of HBM per device.

v0:
```python
import jax
import jax.numpy as jnp
from jax import lax
from jax.sharding import Mesh
from jax.sharding import PartitionSpec as P

ITERS = 3
LEVELS = 3
SWEEPS = 2
BOTTOM = 4
GX = ("gx_0", "gx_1", "gx_2")
GY = ("gy_0", "gy_1")
GX_GY = ("gx_0", "gx_1", "gx_2", "gy_0", "gy_1")
relaxation = 0.7
center_weight = 26.0


def with_halo(block, sides, width):
    for axis, dim in sides:
        count = lax.axis_size(axis)
        forward = [(i, i + 1) for i in range(count - 1)]
        backward = [(target, source) for source, target in forward]
        low = lax.ppermute(
            lax.slice_in_dim(block, block.shape[dim] - width, None, axis=dim), axis, forward
        )
        high = lax.ppermute(lax.slice_in_dim(block, 0, width, axis=dim), axis, backward)
        block = jnp.concatenate([low, block, high], axis=dim)
    return block


def one_axis_at_a_time(x, axes):
    for axis in axes:
        x = lax.psum(x, axis)
    return x


def neighbours(padded):
    total = padded[:, :, :-2] + padded[:, :, 1:-1] + padded[:, :, 2:]
    total = total[:, :-2] + total[:, 1:-1] + total[:, 2:]
    total = total[:-2] + total[1:-1] + total[2:]
    return total - padded[1:-1, 1:-1, 1:-1]


def coarsen(field):
    first, second, third = field.shape
    return field.reshape(first // 2, 2, second // 2, 2, third // 2, 2).mean(axis=(1, 3, 5))


def prolong(field):
    return jnp.repeat(jnp.repeat(jnp.repeat(field, 2, 0), 2, 1), 2, 2)


def level_diagonals(box_shift):
    result = []
    current = box_shift
    for level in range(LEVELS):
        result.append(center_weight + 4.0**level * current)
        if level + 1 < LEVELS:
            current = coarsen(current)
    return result


def sweep(guess, source, diag):
    return guess + relaxation * (source - (diag * guess - neighbours(jnp.pad(guess, 1)))) / diag


def vcycle(rhs, diags, level):
    diag = diags[level]
    source = 4.0**level * rhs
    count = BOTTOM if level == LEVELS - 1 else SWEEPS
    guess = relaxation * source / diag
    for turn in range(count - 1):
        guess = sweep(guess, source, diag)
    if level < LEVELS - 1:
        leftover = (source - (diag * guess - neighbours(jnp.pad(guess, 1)))) / 4.0**level
        guess = guess + prolong(vcycle(coarsen(leftover), diags, level + 1))
        for turn in range(SWEEPS):
            guess = sweep(guess, source, diag)
    return guess


def fold_band(padded, dim, width):
    length = padded.shape[dim]
    core = lax.slice_in_dim(padded, 2 * width, length - 2 * width, axis=dim)
    inner = core.shape[dim]
    lower = lax.slice_in_dim(padded, 0, width, axis=dim)
    upper = lax.slice_in_dim(padded, length - width, length, axis=dim)
    head = lax.slice_in_dim(core, 0, width, axis=dim) + lower
    middle = lax.slice_in_dim(core, width, inner - width, axis=dim)
    tail = lax.slice_in_dim(core, inner - width, inner, axis=dim) + upper
    return jnp.concatenate([head, middle, tail], axis=dim)


def on_device(right_side, shift):
    cells_x = right_side.shape[0]
    cells_y = right_side.shape[1]
    total_x = cells_x * lax.axis_size(GX)
    total_y = cells_y * lax.axis_size(GY)

    def extend(field):
        return with_halo(field, ((GX, 0), (GY, 1)), 2)

    shift_box = extend(shift)
    diags = level_diagonals(shift_box)
    rows = lax.axis_index(GX) * cells_x - 2 + jnp.arange(cells_x + 4, dtype=jnp.int32)
    cols = lax.axis_index(GY) * cells_y - 2 + jnp.arange(cells_y + 4, dtype=jnp.int32)
    row_ok = ((rows >= 0) & (rows < total_x)).astype(jnp.float32)
    col_ok = ((cols >= 0) & (cols < total_y)).astype(jnp.float32)
    grid_mask = row_ok[:, None, None] * col_ok[None, :, None]
    widths = ((1, 1), (1, 1), (0, 0))
    shift_grown = jnp.pad(shift_box, widths)

    def precondition_image(residual):
        local = vcycle(extend(residual), diags, 0) * grid_mask
        grown = jnp.pad(local, widths)
        image_local = (center_weight + shift_grown) * grown - neighbours(jnp.pad(grown, 1))
        stacked = jnp.stack([grown, image_local])
        returned = with_halo(stacked, ((GX, 1), (GY, 2)), 3)
        folded = fold_band(fold_band(returned, 1, 3), 2, 3)
        return (folded[0], folded[1])

    solution_field = jnp.zeros_like(right_side)
    residual = right_side

    def paired_sums(residual, precond, image):
        return (
            one_axis_at_a_time(jnp.sum(residual * precond), GX_GY),
            one_axis_at_a_time(jnp.sum(image * precond), GX_GY),
        )

    precond, image = precondition_image(residual)
    rz_now, product = paired_sums(residual, precond, image)
    alpha = rz_now / product
    direction, along = (precond, image)
    for step in range(ITERS):
        solution_field = solution_field + alpha * direction
        residual = residual - alpha * along
        if step + 1 < ITERS:
            precond, image = precondition_image(residual)
            rz_next, product = paired_sums(residual, precond, image)
            ratio = rz_next / rz_now
            alpha = rz_next / (product - ratio * rz_next / alpha)
            direction = precond + ratio * direction
            along = image + ratio * along
            rz_now = rz_next
    return (solution_field, residual)


def solution(mesh):
    split = Mesh(mesh.devices.reshape(2, 4, 2, 4, 2), ("gx_0", "gx_1", "gx_2", "gy_0", "gy_1"))
    in_specs = (P(GX, GY, None), P(GX, GY, None))
    out_specs = (P(GX, GY, None), P(GX, GY, None))
    return jax.shard_map(
        on_device, mesh=split, in_specs=in_specs, out_specs=out_specs, check_vma=False
    )
```

profile of v0, /device:TPU:42, one launch (start us, length us, event | category | flops | bytes accessed | tf_op | source)
XLA Modules:
  0.0 480.6 jit_solution(9280216936747103945)
XLA Ops:
  16.2 4.3 collective-permute-start.2
  28.0 4.8 %collective-permute-start.7 = (f32[20,2,128]{2,1,0:T(2,128)S(1)}, f32[20,2,128]{2,1,0:T(2,128)S(1)}, u32[]{:S(2)}, u32[]{:S(2)}) collective-permute-start(f32[20,2,128]{2,1,0:T(2,128)S(1)} %get-tuple-element.75), channel_id=1, source_target_pairs={{1,0},{2,1},{3,2},{4,3},{5,4},{6,5},{7,6},{9,8},{10,9},{11,10},{12... | collective-permute-start | bytes 61448 | tf_op jit(solution)/shard_map/ppermute | solution.py:26
  37.0 25.3 %reshape.131 = f32[10,2,18,2,64,2]{5,4,3,2,1,0:T(8,128)} reshape(f32[20,36,128]{2,1,0:T(8,128)S(1)} %fusion.95) | data formatting | bytes 737280 | tf_op jit(solution)/shard_map/reshape | solution.py:46
  62.3 25.2 %reshape.132 = f32[10,2,18,2,64,2]{5,4,3,2,1,0:T(8,128)} reshape(f32[20,36,128]{2,1,0:T(8,128)S(1)} %get-tuple-element.68) | data formatting | bytes 737280 | tf_op jit(solution)/shard_map/reshape | solution.py:46
  87.5 9.1 %reduce_sum.126 = f32[10,18,64]{2,1,0:T(8,128)S(1)} reduce(f32[10,2,18,2,64,2]{5,4,3,2,1,0:T(8,128)} %reshape.131, f32[]{:T(128)} %constant.67.clone.1), dimensions={1,3,5}, to_apply=%region_0.0 | reduce | flops 80640 | bytes 414724 | tf_op jit(solution)/shard_map/reduce_sum | solution.py:46
  96.6 9.1 %reduce_sum.127 = f32[10,18,64]{2,1,0:T(8,128)S(1)} reduce(f32[10,2,18,2,64,2]{5,4,3,2,1,0:T(8,128)} %reshape.132, f32[]{:T(128)} %constant.67.clone.1), dimensions={1,3,5}, to_apply=%region_1.0 | reduce | flops 80640 | bytes 414724 | tf_op jit(solution)/shard_map/reduce_sum | solution.py:46
  108.0 4.0 reshape.133
  112.3 4.2 div.159
  133.1 5.8 %collective-permute-start.10 = (f32[2,28,3,128]{3,0,2,1:T(2,128)S(1)}, f32[2,28,3,128]{3,0,2,1:T(2,128)S(1)}, u32[]{:S(2)}, u32[]{:S(2)}) collective-permute-start(f32[2,28,3,128]{3,0,2,1:T(2,128)S(1)} %get-tuple-element.48), channel_id=1, source_target_pairs={{0,1},{1,2},{2,3},{3,4},{4,5},{5,6},{6,7},{8,9},{9,10},{10,11},{11... | collective-permute-start | bytes 258056 | tf_op jit(solution)/shard_map/ppermute | solution.py:23
  142.1 4.9 %collective-permute-done.11 = f32[2,28,3,128]{3,0,2,1:T(2,128)S(1)} collective-permute-done((f32[2,28,3,128]{3,0,2,1:T(2,128)S(1)}, f32[2,28,3,128]{3,0,2,1:T(2,128)S(1)}, u32[]{:S(2)}, u32[]{:S(2)}) %collective-permute-start.11) | collective-permute-done | bytes 86048 | tf_op jit(solution)/shard_map/ppermute | solution.py:26
  151.3 5.6 %all-reduce.54 = (f32[]{:T(128)}, f32[]{:T(128)}) all-reduce(f32[]{:T(128)} %get-tuple-element.11, f32[]{:T(128)} %get-tuple-element.10), channel_id=1, replica_groups=mesh['gx_0'=2,'gx_1'=4,'gx_2'=2,'gy_0'=4,'gy_1'=2] {'gx_0'}, use_global_device_ids=true, to_apply=%region_5.6 | all-reduce | flops 2 | bytes 16 | tf_op jit(solution)/shard_map/psum | solution.py:33
  156.8 18.0 %all-reduce.45 = (f32[]{:T(128)}, f32[]{:T(128)}) all-reduce(f32[]{:T(128)} %get-tuple-element.40, f32[]{:T(128)} %get-tuple-element.41), channel_id=1, replica_groups=mesh['gx_0'=2,'gx_1'=4,'gx_2'=2,'gy_0'=4,'gy_1'=2] {'gx_1'}, use_global_device_ids=true, to_apply=%region_6.7 | all-reduce | flops 2 | bytes 16 | tf_op jit(solution)/shard_map/psum | solution.py:33
  177.9 9.0 %all-reduce.42 = (f32[]{:T(128)}, f32[]{:T(128)}) all-reduce(f32[]{:T(128)} %get-tuple-element.34, f32[]{:T(128)} %get-tuple-element.35), channel_id=1, replica_groups=mesh['gx_0'=2,'gx_1'=4,'gx_2'=2,'gy_0'=4,'gy_1'=2] {'gy_0'}, use_global_device_ids=true, to_apply=%region_8.9 | all-reduce | flops 2 | bytes 16 | tf_op jit(solution)/shard_map/psum | solution.py:33
  186.9 7.1 %all-reduce.48 = (f32[]{:T(128)}, f32[]{:T(128)}) all-reduce(f32[]{:T(128)} %get-tuple-element.16, f32[]{:T(128)} %get-tuple-element.17), channel_id=1, replica_groups=mesh['gx_0'=2,'gx_1'=4,'gx_2'=2,'gy_0'=4,'gy_1'=2] {'gy_1'}, use_global_device_ids=true, to_apply=%region_9.10 | all-reduce | flops 2 | bytes 16 | tf_op jit(solution)/shard_map/psum | solution.py:33
  205.7 5.0 %collective-permute-start.15 = (f32[20,2,128]{2,1,0:T(2,128)S(1)}, f32[20,2,128]{2,1,0:T(2,128)S(1)}, u32[]{:S(2)}, u32[]{:S(2)}) collective-permute-start(f32[20,2,128]{2,1,0:T(2,128)S(1)} %get-tuple-element.73), channel_id=1, source_target_pairs={{1,0},{2,1},{3,2},{4,3},{5,4},{6,5},{7,6},{9,8},{10,9},{11,10},{12... | collective-permute-start | bytes 61448 | tf_op jit(solution)/shard_map/ppermute | solution.py:26
  214.3 25.5 %reshape.140 = f32[10,2,18,2,64,2]{5,4,3,2,1,0:T(8,128)} reshape(f32[20,36,128]{2,1,0:T(8,128)S(1)} %fusion.74) | data formatting | bytes 737280 | tf_op jit(solution)/shard_map/reshape | solution.py:46
  239.7 9.1 %reduce_sum.132 = f32[10,18,64]{2,1,0:T(8,128)S(1)} reduce(f32[10,2,18,2,64,2]{5,4,3,2,1,0:T(8,128)} %reshape.140, f32[]{:T(128)} %constant.67.clone.1), dimensions={1,3,5}, to_apply=%region_16.17 | reduce | flops 80640 | bytes 414724 | tf_op jit(solution)/shard_map/reduce_sum | solution.py:46
  249.4 4.7 reshape.141
  273.6 4.6 collective-permute-start.18
  290.0 5.6 %all-reduce.53 = (f32[]{:T(128)}, f32[]{:T(128)}) all-reduce(f32[]{:T(128)} %get-tuple-element.9, f32[]{:T(128)} %get-tuple-element.8), channel_id=1, replica_groups=mesh['gx_0'=2,'gx_1'=4,'gx_2'=2,'gy_0'=4,'gy_1'=2] {'gx_0'}, use_global_device_ids=true, to_apply=%region_19.20 | all-reduce | flops 2 | bytes 16 | tf_op jit(solution)/shard_map/psum | solution.py:33
  295.6 12.6 %all-reduce.44 = (f32[]{:T(128)}, f32[]{:T(128)}) all-reduce(f32[]{:T(128)} %get-tuple-element.38, f32[]{:T(128)} %get-tuple-element.39), channel_id=1, replica_groups=mesh['gx_0'=2,'gx_1'=4,'gx_2'=2,'gy_0'=4,'gy_1'=2] {'gx_1'}, use_global_device_ids=true, to_apply=%region_20.21 | all-reduce | flops 2 | bytes 16 | tf_op jit(solution)/shard_map/psum | solution.py:33
  311.2 10.2 %all-reduce.41 = (f32[]{:T(128)}, f32[]{:T(128)}) all-reduce(f32[]{:T(128)} %get-tuple-element.32, f32[]{:T(128)} %get-tuple-element.33), channel_id=1, replica_groups=mesh['gx_0'=2,'gx_1'=4,'gx_2'=2,'gy_0'=4,'gy_1'=2] {'gy_0'}, use_global_device_ids=true, to_apply=%region_22.23 | all-reduce | flops 2 | bytes 16 | tf_op jit(solution)/shard_map/psum | solution.py:33
  321.4 7.0 %all-reduce.47 = (f32[]{:T(128)}, f32[]{:T(128)}) all-reduce(f32[]{:T(128)} %get-tuple-element.14, f32[]{:T(128)} %get-tuple-element.15), channel_id=1, replica_groups=mesh['gx_0'=2,'gx_1'=4,'gx_2'=2,'gy_0'=4,'gy_1'=2] {'gy_1'}, use_global_device_ids=true, to_apply=%region_23.24 | all-reduce | flops 2 | bytes 16 | tf_op jit(solution)/shard_map/psum | solution.py:33
  343.5 5.0 %collective-permute-start.23 = (f32[20,2,128]{2,1,0:T(2,128)S(1)}, f32[20,2,128]{2,1,0:T(2,128)S(1)}, u32[]{:S(2)}, u32[]{:S(2)}) collective-permute-start(f32[20,2,128]{2,1,0:T(2,128)S(1)} %get-tuple-element.71), channel_id=1, source_target_pairs={{1,0},{2,1},{3,2},{4,3},{5,4},{6,5},{7,6},{9,8},{10,9},{11,10},{12... | collective-permute-start | bytes 61448 | tf_op jit(solution)/shard_map/ppermute | solution.py:26
  352.8 26.0 %reshape.148 = f32[10,2,18,2,64,2]{5,4,3,2,1,0:T(8,128)} reshape(f32[20,36,128]{2,1,0:T(8,128)} %fusion.53) | data formatting | bytes 737280 | tf_op jit(solution)/shard_map/reshape | solution.py:46
  378.8 9.1 %reduce_sum.136 = f32[10,18,64]{2,1,0:T(8,128)S(1)} reduce(f32[10,2,18,2,64,2]{5,4,3,2,1,0:T(8,128)} %reshape.148, f32[]{:T(128)} %constant.67.clone.1), dimensions={1,3,5}, to_apply=%region_30.31 | reduce | flops 80640 | bytes 414724 | tf_op jit(solution)/shard_map/reduce_sum | solution.py:46
  388.5 4.7 reshape.149
  424.4 4.7 collective-permute-start.27
  436.0 5.6 %all-reduce.52 = (f32[]{:T(128)}, f32[]{:T(128)}) all-reduce(f32[]{:T(128)} %get-tuple-element.7, f32[]{:T(128)} %get-tuple-element.6), channel_id=1, replica_groups=mesh['gx_0'=2,'gx_1'=4,'gx_2'=2,'gy_0'=4,'gy_1'=2] {'gx_0'}, use_global_device_ids=true, to_apply=%region_33.34 | all-reduce | flops 2 | bytes 16 | tf_op jit(solution)/shard_map/psum | solution.py:33
  441.6 12.6 %all-reduce.43 = (f32[]{:T(128)}, f32[]{:T(128)}) all-reduce(f32[]{:T(128)} %get-tuple-element.36, f32[]{:T(128)} %get-tuple-element.37), channel_id=1, replica_groups=mesh['gx_0'=2,'gx_1'=4,'gx_2'=2,'gy_0'=4,'gy_1'=2] {'gx_1'}, use_global_device_ids=true, to_apply=%region_34.35 | all-reduce | flops 2 | bytes 16 | tf_op jit(solution)/shard_map/psum | solution.py:33
  457.3 11.2 %all-reduce.40 = (f32[]{:T(128)}, f32[]{:T(128)}) all-reduce(f32[]{:T(128)} %get-tuple-element.30, f32[]{:T(128)} %get-tuple-element.31), channel_id=1, replica_groups=mesh['gx_0'=2,'gx_1'=4,'gx_2'=2,'gy_0'=4,'gy_1'=2] {'gy_0'}, use_global_device_ids=true, to_apply=%region_36.37 | all-reduce | flops 2 | bytes 16 | tf_op jit(solution)/shard_map/psum | solution.py:33
  468.5 7.1 %all-reduce.46 = (f32[]{:T(128)}, f32[]{:T(128)}) all-reduce(f32[]{:T(128)} %get-tuple-element.12, f32[]{:T(128)} %get-tuple-element.13), channel_id=1, replica_groups=mesh['gx_0'=2,'gx_1'=4,'gx_2'=2,'gy_0'=4,'gy_1'=2] {'gy_1'}, use_global_device_ids=true, to_apply=%region_37.38 | all-reduce | flops 2 | bytes 16 | tf_op jit(solution)/shard_map/psum | solution.py:33
  (336 shorter events, 161.8 us)
Async XLA Ops:
  0.6 23.9 %copy-start.17 = (f32[16,32,128]{2,1,0:T(8,128)S(1)}, f32[16,32,128]{2,1,0:T(8,128)}, u32[]{:S(2)}) copy-start(f32[16,32,128]{2,1,0:T(8,128)} %param.3) | copy-start | bytes 786436
  1.5 23.1 %collective-permute-start.5 = (f32[2,32,128]{2,1,0:T(8,128)S(1)}, f32[2,32,128]{2,1,0:T(8,128)S(1)}, u32[]{:S(2)}, u32[]{:S(2)}) collective-permute-start(f32[2,32,128]{2,1,0:T(8,128)S(1)} %get-tuple-element.82), channel_id=1, source_target_pairs={{8,0},{16,8},{24,16},{32,24},{40,32},{48,40},{56,48},{64,56},{72,6... | collective-permute-start | bytes 98312 | tf_op jit(solution)/shard_map/ppermute | solution.py:26
  3.4 21.1 %collective-permute-start.4 = (f32[2,32,128]{2,1,0:T(8,128)S(1)}, f32[2,32,128]{2,1,0:T(8,128)S(1)}, u32[]{:S(2)}, u32[]{:S(2)}) collective-permute-start(f32[2,32,128]{2,1,0:T(8,128)S(1)} %get-tuple-element.83), channel_id=1, source_target_pairs={{0,8},{8,16},{16,24},{24,32},{32,40},{40,48},{48,56},{56,64},{64,7... | collective-permute-start | bytes 98312 | tf_op jit(solution)/shard_map/ppermute | solution.py:23
  6.6 9.6 %collective-permute-start.1 = (f32[2,32,128]{2,1,0:T(8,128)S(1)}, f32[2,32,128]{2,1,0:T(8,128)S(1)}, u32[]{:S(2)}, u32[]{:S(2)}) collective-permute-start(f32[2,32,128]{2,1,0:T(8,128)S(1)} %get-tuple-element.84), channel_id=1, source_target_pairs={{8,0},{16,8},{24,16},{32,24},{40,32},{48,40},{56,48},{64,56},{72,6... | collective-permute-start | bytes 98312 | tf_op jit(solution)/shard_map/ppermute | solution.py:26
  9.7 5.4 %collective-permute-start = (f32[2,32,128]{2,1,0:T(8,128)S(1)}, f32[2,32,128]{2,1,0:T(8,128)S(1)}, u32[]{:S(2)}, u32[]{:S(2)}) collective-permute-start(f32[2,32,128]{2,1,0:T(8,128)S(1)} %get-tuple-element.85), channel_id=1, source_target_pairs={{0,8},{8,16},{16,24},{24,32},{32,40},{40,48},{48,56},{56,64},{64,7... | collective-permute-start | bytes 98312 | tf_op jit(solution)/shard_map/ppermute | solution.py:23
  16.2 20.2 %copy-start.2 = (f32[20,32,128]{2,1,0:T(8,128)}, f32[20,32,128]{2,1,0:T(8,128)S(1)}, u32[]{:S(2)}) copy-start(f32[20,32,128]{2,1,0:T(8,128)S(1)} %constant_dynamic-update-slice_fusion) | copy-start | bytes 983044
  16.2 16.7 %collective-permute-start.2 = (f32[20,2,128]{2,1,0:T(2,128)S(1)}, f32[20,2,128]{2,1,0:T(2,128)S(1)}, u32[]{:S(2)}, u32[]{:S(2)}) collective-permute-start(f32[20,2,128]{2,1,0:T(2,128)S(1)} %get-tuple-element.76), channel_id=1, source_target_pairs={{0,1},{1,2},{2,3},{3,4},{4,5},{5,6},{6,7},{8,9},{9,10},{10,11},{11... | collective-permute-start | bytes 61448 | tf_op jit(solution)/shard_map/ppermute | solution.py:23
  20.5 12.4 %collective-permute-start.3 = (f32[20,2,128]{2,1,0:T(2,128)S(1)}, f32[20,2,128]{2,1,0:T(2,128)S(1)}, u32[]{:S(2)}, u32[]{:S(2)}) collective-permute-start(f32[20,2,128]{2,1,0:T(2,128)S(1)} %get-tuple-element.77), channel_id=1, source_target_pairs={{1,0},{2,1},{3,2},{4,3},{5,4},{6,5},{7,6},{9,8},{10,9},{11,10},{12... | collective-permute-start | bytes 61448 | tf_op jit(solution)/shard_map/ppermute | solution.py:26
  24.6 8.4 %collective-permute-start.6 = (f32[20,2,128]{2,1,0:T(2,128)S(1)}, f32[20,2,128]{2,1,0:T(2,128)S(1)}, u32[]{:S(2)}, u32[]{:S(2)}) collective-permute-start(f32[20,2,128]{2,1,0:T(2,128)S(1)} %get-tuple-element.74), channel_id=1, source_target_pairs={{0,1},{1,2},{2,3},{3,4},{4,5},{5,6},{6,7},{8,9},{9,10},{10,11},{11... | collective-permute-start | bytes 61448 | tf_op jit(solution)/shard_map/ppermute | solution.py:23
  28.0 7.2 %collective-permute-start.7 = (f32[20,2,128]{2,1,0:T(2,128)S(1)}, f32[20,2,128]{2,1,0:T(2,128)S(1)}, u32[]{:S(2)}, u32[]{:S(2)}) collective-permute-start(f32[20,2,128]{2,1,0:T(2,128)S(1)} %get-tuple-element.75), channel_id=1, source_target_pairs={{1,0},{2,1},{3,2},{4,3},{5,4},{6,5},{7,6},{9,8},{10,9},{11,10},{12... | collective-permute-start | bytes 61448 | tf_op jit(solution)/shard_map/ppermute | solution.py:26
  32.9 89.5 %copy-start.18 = (f32[20,36]{1,0:T(8,128)}, f32[20,36]{1,0:T(8,128)S(1)}, u32[]{:S(2)}) copy-start(f32[20,36]{1,0:T(8,128)S(1)} %broadcast_multiply_fusion.1) | copy-start | bytes 8644
  35.3 26.9 %copy-start = (f32[20,36,128]{2,1,0:T(8,128)}, f32[20,36,128]{2,1,0:T(8,128)S(1)}, u32[]{:S(2)}) copy-start(f32[20,36,128]{2,1,0:T(8,128)S(1)} %get-tuple-element.68) | copy-start | bytes 1105924
  125.0 6.1 %collective-permute-start.8 = (f32[2,3,38,128]{3,0,2,1:T(2,128)S(1)}, f32[2,3,38,128]{3,0,2,1:T(2,128)S(1)}, u32[]{:S(2)}, u32[]{:S(2)}) collective-permute-start(f32[2,3,38,128]{3,0,2,1:T(2,128)S(1)} %get-tuple-element.60), channel_id=1, source_target_pairs={{0,8},{8,16},{16,24},{24,32},{32,40},{40,48},{48,56},{56,64},{64,7... | collective-permute-start | bytes 350216 | tf_op jit(solution)/shard_map/ppermute | solution.py:23
  127.0 6.0 %collective-permute-start.9 = (f32[2,3,38,128]{3,0,2,1:T(2,128)S(1)}, f32[2,3,38,128]{3,0,2,1:T(2,128)S(1)}, u32[]{:S(2)}, u32[]{:S(2)}) collective-permute-start(f32[2,3,38,128]{3,0,2,1:T(2,128)S(1)} %get-tuple-element.61), channel_id=1, source_target_pairs={{8,0},{16,8},{24,16},{32,24},{40,32},{48,40},{56,48},{64,56},{72,6... | collective-permute-start | bytes 350216 | tf_op jit(solution)/shard_map/ppermute | solution.py:26
  133.1 9.0 %collective-permute-start.10 = (f32[2,28,3,128]{3,0,2,1:T(2,128)S(1)}, f32[2,28,3,128]{3,0,2,1:T(2,128)S(1)}, u32[]{:S(2)}, u32[]{:S(2)}) collective-permute-start(f32[2,28,3,128]{3,0,2,1:T(2,128)S(1)} %get-tuple-element.48), channel_id=1, source_target_pairs={{0,1},{1,2},{2,3},{3,4},{4,5},{5,6},{6,7},{8,9},{9,10},{10,11},{11... | collective-permute-start | bytes 258056 | tf_op jit(solution)/shard_map/ppermute | solution.py:23
  139.0 8.1 %collective-permute-start.11 = (f32[2,28,3,128]{3,0,2,1:T(2,128)S(1)}, f32[2,28,3,128]{3,0,2,1:T(2,128)S(1)}, u32[]{:S(2)}, u32[]{:S(2)}) collective-permute-start(f32[2,28,3,128]{3,0,2,1:T(2,128)S(1)} %get-tuple-element.49), channel_id=1, source_target_pairs={{1,0},{2,1},{3,2},{4,3},{5,4},{6,5},{7,6},{9,8},{10,9},{11,10},{12... | collective-permute-start | bytes 258056 | tf_op jit(solution)/shard_map/ppermute | solution.py:26
  195.2 5.6 %collective-permute-start.12 = (f32[2,32,128]{2,1,0:T(8,128)S(1)}, f32[2,32,128]{2,1,0:T(8,128)S(1)}, u32[]{:S(2)}, u32[]{:S(2)}) collective-permute-start(f32[2,32,128]{2,1,0:T(8,128)S(1)} %get-tuple-element.80), channel_id=1, source_target_pairs={{0,8},{8,16},{16,24},{24,32},{32,40},{40,48},{48,56},{56,64},{64,7... | collective-permute-start | bytes 98312 | tf_op jit(solution)/shard_map/ppermute | solution.py:23
  197.2 5.2 %collective-permute-start.13 = (f32[2,32,128]{2,1,0:T(8,128)S(1)}, f32[2,32,128]{2,1,0:T(8,128)S(1)}, u32[]{:S(2)}, u32[]{:S(2)}) collective-permute-start(f32[2,32,128]{2,1,0:T(8,128)S(1)} %get-tuple-element.81), channel_id=1, source_target_pairs={{8,0},{16,8},{24,16},{32,24},{40,32},{48,40},{56,48},{64,56},{72,6... | collective-permute-start | bytes 98312 | tf_op jit(solution)/shard_map/ppermute | solution.py:26
  202.4 8.3 %collective-permute-start.14 = (f32[20,2,128]{2,1,0:T(2,128)S(1)}, f32[20,2,128]{2,1,0:T(2,128)S(1)}, u32[]{:S(2)}, u32[]{:S(2)}) collective-permute-start(f32[20,2,128]{2,1,0:T(2,128)S(1)} %get-tuple-element.72), channel_id=1, source_target_pairs={{0,1},{1,2},{2,3},{3,4},{4,5},{5,6},{6,7},{8,9},{9,10},{10,11},{11... | collective-permute-start | bytes 61448 | tf_op jit(solution)/shard_map/ppermute | solution.py:23
  205.7 7.2 %collective-permute-start.15 = (f32[20,2,128]{2,1,0:T(2,128)S(1)}, f32[20,2,128]{2,1,0:T(2,128)S(1)}, u32[]{:S(2)}, u32[]{:S(2)}) collective-permute-start(f32[20,2,128]{2,1,0:T(2,128)S(1)} %get-tuple-element.73), channel_id=1, source_target_pairs={{1,0},{2,1},{3,2},{4,3},{5,4},{6,5},{7,6},{9,8},{10,9},{11,10},{12... | collective-permute-start | bytes 61448 | tf_op jit(solution)/shard_map/ppermute | solution.py:26
  265.5 6.1 %collective-permute-start.16 = (f32[2,3,38,128]{3,0,2,1:T(2,128)S(1)}, f32[2,3,38,128]{3,0,2,1:T(2,128)S(1)}, u32[]{:S(2)}, u32[]{:S(2)}) collective-permute-start(f32[2,3,38,128]{3,0,2,1:T(2,128)S(1)} %get-tuple-element.58), channel_id=1, source_target_pairs={{0,8},{8,16},{16,24},{24,32},{32,40},{40,48},{48,56},{56,64},{64,7... | collective-permute-start | bytes 350216 | tf_op jit(solution)/shard_map/ppermute | solution.py:23
  267.4 6.0 %collective-permute-start.17 = (f32[2,3,38,128]{3,0,2,1:T(2,128)S(1)}, f32[2,3,38,128]{3,0,2,1:T(2,128)S(1)}, u32[]{:S(2)}, u32[]{:S(2)}) collective-permute-start(f32[2,3,38,128]{3,0,2,1:T(2,128)S(1)} %get-tuple-element.59), channel_id=1, source_target_pairs={{8,0},{16,8},{24,16},{32,24},{40,32},{48,40},{56,48},{64,56},{72,6... | collective-permute-start | bytes 350216 | tf_op jit(solution)/shard_map/ppermute | solution.py:26
  273.6 8.8 %collective-permute-start.18 = (f32[2,28,3,128]{3,0,2,1:T(2,128)S(1)}, f32[2,28,3,128]{3,0,2,1:T(2,128)S(1)}, u32[]{:S(2)}, u32[]{:S(2)}) collective-permute-start(f32[2,28,3,128]{3,0,2,1:T(2,128)S(1)} %get-tuple-element.46), channel_id=1, source_target_pairs={{0,1},{1,2},{2,3},{3,4},{4,5},{5,6},{6,7},{8,9},{9,10},{10,11},{11... | collective-permute-start | bytes 258056 | tf_op jit(solution)/shard_map/ppermute | solution.py:23
  278.2 7.9 %collective-permute-start.19 = (f32[2,28,3,128]{3,0,2,1:T(2,128)S(1)}, f32[2,28,3,128]{3,0,2,1:T(2,128)S(1)}, u32[]{:S(2)}, u32[]{:S(2)}) collective-permute-start(f32[2,28,3,128]{3,0,2,1:T(2,128)S(1)} %get-tuple-element.47), channel_id=1, source_target_pairs={{1,0},{2,1},{3,2},{4,3},{5,4},{6,5},{7,6},{9,8},{10,9},{11,10},{12... | collective-permute-start | bytes 258056 | tf_op jit(solution)/shard_map/ppermute | solution.py:26
  333.0 5.6 %collective-permute-start.20 = (f32[2,32,128]{2,1,0:T(8,128)S(1)}, f32[2,32,128]{2,1,0:T(8,128)S(1)}, u32[]{:S(2)}, u32[]{:S(2)}) collective-permute-start(f32[2,32,128]{2,1,0:T(8,128)S(1)} %get-tuple-element.78), channel_id=1, source_target_pairs={{0,8},{8,16},{16,24},{24,32},{32,40},{40,48},{48,56},{56,64},{64,7... | collective-permute-start | bytes 98312 | tf_op jit(solution)/shard_map/ppermute | solution.py:23
  334.9 5.2 %collective-permute-start.21 = (f32[2,32,128]{2,1,0:T(8,128)S(1)}, f32[2,32,128]{2,1,0:T(8,128)S(1)}, u32[]{:S(2)}, u32[]{:S(2)}) collective-permute-start(f32[2,32,128]{2,1,0:T(8,128)S(1)} %get-tuple-element.79), channel_id=1, source_target_pairs={{8,0},{16,8},{24,16},{32,24},{40,32},{48,40},{56,48},{64,56},{72,6... | collective-permute-start | bytes 98312 | tf_op jit(solution)/shard_map/ppermute | solution.py:26
  340.2 8.3 %collective-permute-start.22 = (f32[20,2,128]{2,1,0:T(2,128)S(1)}, f32[20,2,128]{2,1,0:T(2,128)S(1)}, u32[]{:S(2)}, u32[]{:S(2)}) collective-permute-start(f32[20,2,128]{2,1,0:T(2,128)S(1)} %get-tuple-element.70), channel_id=1, source_target_pairs={{0,1},{1,2},{2,3},{3,4},{4,5},{5,6},{6,7},{8,9},{9,10},{10,11},{11... | collective-permute-start | bytes 61448 | tf_op jit(solution)/shard_map/ppermute | solution.py:23
  343.5 7.2 %collective-permute-start.23 = (f32[20,2,128]{2,1,0:T(2,128)S(1)}, f32[20,2,128]{2,1,0:T(2,128)S(1)}, u32[]{:S(2)}, u32[]{:S(2)}) collective-permute-start(f32[20,2,128]{2,1,0:T(2,128)S(1)} %get-tuple-element.71), channel_id=1, source_target_pairs={{1,0},{2,1},{3,2},{4,3},{5,4},{6,5},{7,6},{9,8},{10,9},{11,10},{12... | collective-permute-start | bytes 61448 | tf_op jit(solution)/shard_map/ppermute | solution.py:26
  412.7 6.1 %collective-permute-start.24 = (f32[2,3,38,128]{3,0,2,1:T(2,128)S(1)}, f32[2,3,38,128]{3,0,2,1:T(2,128)S(1)}, u32[]{:S(2)}, u32[]{:S(2)}) collective-permute-start(f32[2,3,38,128]{3,0,2,1:T(2,128)S(1)} %get-tuple-element.56), channel_id=1, source_target_pairs={{0,8},{8,16},{16,24},{24,32},{32,40},{40,48},{48,56},{56,64},{64,7... | collective-permute-start | bytes 350216 | tf_op jit(solution)/shard_map/ppermute | solution.py:23
  414.7 6.0 %collective-permute-start.25 = (f32[2,3,38,128]{3,0,2,1:T(2,128)S(1)}, f32[2,3,38,128]{3,0,2,1:T(2,128)S(1)}, u32[]{:S(2)}, u32[]{:S(2)}) collective-permute-start(f32[2,3,38,128]{3,0,2,1:T(2,128)S(1)} %get-tuple-element.57), channel_id=1, source_target_pairs={{8,0},{16,8},{24,16},{32,24},{40,32},{48,40},{56,48},{64,56},{72,6... | collective-permute-start | bytes 350216 | tf_op jit(solution)/shard_map/ppermute | solution.py:26
  420.8 8.8 %collective-permute-start.26 = (f32[2,28,3,128]{3,0,2,1:T(2,128)S(1)}, f32[2,28,3,128]{3,0,2,1:T(2,128)S(1)}, u32[]{:S(2)}, u32[]{:S(2)}) collective-permute-start(f32[2,28,3,128]{3,0,2,1:T(2,128)S(1)} %get-tuple-element.44), channel_id=1, source_target_pairs={{0,1},{1,2},{2,3},{3,4},{4,5},{5,6},{6,7},{8,9},{9,10},{10,11},{11... | collective-permute-start | bytes 258056 | tf_op jit(solution)/shard_map/ppermute | solution.py:23
  424.4 7.9 %collective-permute-start.27 = (f32[2,28,3,128]{3,0,2,1:T(2,128)S(1)}, f32[2,28,3,128]{3,0,2,1:T(2,128)S(1)}, u32[]{:S(2)}, u32[]{:S(2)}) collective-permute-start(f32[2,28,3,128]{3,0,2,1:T(2,128)S(1)} %get-tuple-element.45), channel_id=1, source_target_pairs={{1,0},{2,1},{3,2},{4,3},{5,4},{6,5},{7,6},{9,8},{10,9},{11,10},{12... | collective-permute-start | bytes 258056 | tf_op jit(solution)/shard_map/ppermute | solution.py:26
  (17 other events, 29.4 us)
where the time goes:
time: 490 us; the launch traced here: 481 us
  local copies, waits for them, and re-layouts  148 us (30%)
  blocking collectives  121 us (25%)
  starting transfers between devices  95.2 us (19%)
  other arithmetic  70.9 us (14%)
  waiting for transfers between devices  33.1 us (7%)
  between operations  12.3 us (3%)
    psum x15, blocking collectives, one_axis_at_a_time(): x = lax.psum(x, axis)  121 us
    reshape x7, local copies, waits for them, and re-layouts, coarsen(): field.reshape(first // 2, 2, second // 2, 2, third // 2, 2)  115 us
    ppermute x14, starting transfers between devices, with_halo(): lax.ppermute(lax.slice_in_dim(block, 0, width, axis=dim), axis, backward)  52.7 us
    ppermute x14, starting transfers between devices, with_halo(): lax.ppermute(lax.slice_in_dim(block, block.shape[dim] - width, None, axis...  42.5 us
    reduce_sum x8, other arithmetic, coarsen(): field.reshape(first // 2, 2, second // 2, 2, third // 2, 2)  41.2 us
    ppermute x14, waiting for transfers between devices, with_halo(): lax.ppermute(lax.slice_in_dim(block, 0, width, axis=dim), axis, backward)  26.4 us
    reshape x18, local copies, waits for them, and re-layouts, prolong(): return jnp.repeat(jnp.repeat(jnp.repeat(field, 2, 0), 2, 1), 2, 2)  10.5 us
  transfers between devices with their start and end apart: 28, of which 18 were waited for; matrix products, arithmetic and copies ran while one was open for 0% of the time, Pallas kernels for 0%

commit v1 on v0

--- a/solution.py
+++ b/solution.py
@@ -30,7 +30,7 @@
 
 def one_axis_at_a_time(x, axes):
     for axis in axes:
-        x = lax.psum(x, axis)
+        x = jnp.sum(lax.all_gather(x, axis), axis=0)
     return x
 
 

time: 490 us -> 539 us (1.10)
  local copies, waits for them, and re-layouts: 148 us -> 194 us
  other arithmetic: 70.9 us -> 89.6 us
  blocking collectives: 121 us -> 108 us
    psum x15 -> x0, blocking collectives: 121 us -> none  [one_axis_at_a_time(): x = lax.psum(x, axis)]
    unnamed x0 -> x15, blocking collectives: none -> 108 us
    unnamed x46 -> x103, local copies, waits for them, and re-layouts: 5.49 us -> 49.6 us
    reduce_sum x0 -> x30, other arithmetic: none -> 19 us  [one_axis_at_a_time(): x = jnp.sum(lax.all_gather(x, axis), axis=0)]
  transfers between devices with their start and end apart: 28 -> 28, of which waited for: 18 -> 16; matrix products, arithmetic and copies ran while one was open for 0% -> 0% of each run, Pallas kernels for 0% -> 0%
where the time goes in v1:
time: 539 us; the launch traced here: 530 us
  local copies, waits for them, and re-layouts  194 us (36%)
  blocking collectives  108 us (20%)
  starting transfers between devices  97.4 us (18%)
  other arithmetic  89.6 us (17%)
  waiting for transfers between devices  28.4 us (5%)
  between operations  12.3 us (2%)
    reshape x7, local copies, waits for them, and re-layouts, coarsen(): field.reshape(first // 2, 2, second // 2, 2, third // 2, 2)  114 us
    unnamed x15, blocking collectives  108 us
    ppermute x14, starting transfers between devices, with_halo(): lax.ppermute(lax.slice_in_dim(block, 0, width, axis=dim), axis, backward)  55.8 us
    unnamed x103, local copies, waits for them, and re-layouts  49.6 us
    reduce_sum x8, other arithmetic, coarsen(): field.reshape(first // 2, 2, second // 2, 2, third // 2, 2)  43 us
    ppermute x14, starting transfers between devices, with_halo(): lax.ppermute(lax.slice_in_dim(block, block.shape[dim] - width, None, axis...  41.7 us
    ppermute x14, waiting for transfers between devices, with_halo(): lax.ppermute(lax.slice_in_dim(block, 0, width, axis=dim), axis, backward)  26 us
    reduce_sum x30, other arithmetic, one_axis_at_a_time(): x = jnp.sum(lax.all_gather(x, axis), axis=0)  19 us
  transfers between devices with their start and end apart: 28, of which 16 were waited for; matrix products, arithmetic and copies ran while one was open for 0% of the time, Pallas kernels for 0%

profile of v1, /device:TPU:42, one launch (start us, length us, event | category | flops | bytes accessed | tf_op | source)
XLA Modules:
  0.0 529.5 jit_solution(1044055314973434174)
XLA Ops:
  14.5 4.0 collective-permute-start.6
  18.5 4.2 collective-permute-start.7
  26.0 5.1 collective-permute-start.3
  35.0 25.3 %reshape.131 = f32[10,2,18,2,64,2]{5,4,3,2,1,0:T(8,128)} reshape(f32[20,36,128]{2,1,0:T(8,128)S(1)} %fusion.95) | data formatting | bytes 737280 | tf_op jit(solution)/shard_map/reshape | solution.py:46
  60.3 25.2 %reshape.132 = f32[10,2,18,2,64,2]{5,4,3,2,1,0:T(8,128)} reshape(f32[20,36,128]{2,1,0:T(8,128)S(1)} %get-tuple-element.68) | data formatting | bytes 737280 | tf_op jit(solution)/shard_map/reshape | solution.py:46
  85.5 9.1 %reduce_sum.396 = f32[10,18,64]{2,1,0:T(8,128)S(1)} reduce(f32[10,2,18,2,64,2]{5,4,3,2,1,0:T(8,128)} %reshape.131, f32[]{:T(128)} %constant.67.clone.1), dimensions={1,3,5}, to_apply=%region_0.0 | reduce | flops 80640 | bytes 414724 | tf_op jit(solution)/shard_map/reduce_sum | solution.py:46
  94.6 9.1 %reduce_sum.397 = f32[10,18,64]{2,1,0:T(8,128)S(1)} reduce(f32[10,2,18,2,64,2]{5,4,3,2,1,0:T(8,128)} %reshape.132, f32[]{:T(128)} %constant.67.clone.1), dimensions={1,3,5}, to_apply=%region_1.0 | reduce | flops 80640 | bytes 414724 | tf_op jit(solution)/shard_map/reduce_sum | solution.py:46
  110.0 5.1 div.159
  133.9 6.1 %collective-permute-start.10 = (f32[2,28,3,128]{3,0,2,1:T(2,128)S(1)}, f32[2,28,3,128]{3,0,2,1:T(2,128)S(1)}, u32[]{:S(2)}, u32[]{:S(2)}) collective-permute-start(f32[2,28,3,128]{3,0,2,1:T(2,128)S(1)} %get-tuple-element.48), channel_id=1, source_target_pairs={{0,1},{1,2},{2,3},{3,4},{4,5},{5,6},{6,7},{8,9},{9,10},{10,11},{11... | collective-permute-start | bytes 258056 | tf_op jit(solution)/shard_map/ppermute | solution.py:23
  142.8 5.2 collective-permute-done.11
  155.4 4.9 all-reduce.84
  165.1 14.6 %all-reduce.75 = (f32[4]{0:T(128)S(1)}, f32[4]{0:T(128)S(1)}) all-reduce(f32[4]{0:T(128)S(1)} %dynamic-update-slice.1, f32[4]{0:T(128)S(1)} %dynamic-update-slice.6), channel_id=1, replica_groups=mesh['gx_0'=2,'gx_1'=4,'gx_2'=2,'gy_0'=4,'gy_1'=2] {'gx_1'}, use_global_device_ids=true, to_apply=%add.41 | all-reduce | flops 8 | bytes 64
  191.7 8.4 %all-reduce.72 = (f32[4]{0:T(128)S(1)}, f32[4]{0:T(128)S(1)}) all-reduce(f32[4]{0:T(128)S(1)} %dynamic-update-slice.3, f32[4]{0:T(128)S(1)} %dynamic-update-slice.8), channel_id=1, replica_groups=mesh['gx_0'=2,'gx_1'=4,'gx_2'=2,'gy_0'=4,'gy_1'=2] {'gy_0'}, use_global_device_ids=true, to_apply=%add.43 | all-reduce | flops 8 | bytes 64
  204.1 6.4 %all-reduce.78 = (f32[2]{0:T(128)S(1)}, f32[2]{0:T(128)S(1)}) all-reduce(f32[2]{0:T(128)S(1)} %dynamic-update-slice.4, f32[2]{0:T(128)S(1)} %dynamic-update-slice.9), channel_id=1, replica_groups=mesh['gx_0'=2,'gx_1'=4,'gx_2'=2,'gy_0'=4,'gy_1'=2] {'gy_1'}, use_global_device_ids=true, to_apply=%add.44 | all-reduce | flops 4 | bytes 32
  223.4 5.5 %collective-permute-start.15 = (f32[20,2,128]{2,1,0:T(2,128)S(1)}, f32[20,2,128]{2,1,0:T(2,128)S(1)}, u32[]{:S(2)}, u32[]{:S(2)}) collective-permute-start(f32[20,2,128]{2,1,0:T(2,128)S(1)} %get-tuple-element.73), channel_id=1, source_target_pairs={{1,0},{2,1},{3,2},{4,3},{5,4},{6,5},{7,6},{9,8},{10,9},{11,10},{12... | collective-permute-start | bytes 61448 | tf_op jit(solution)/shard_map/ppermute | solution.py:26
  232.0 25.3 %reshape.140 = f32[10,2,18,2,64,2]{5,4,3,2,1,0:T(8,128)} reshape(f32[20,36,128]{2,1,0:T(8,128)S(1)} %fusion.74) | data formatting | bytes 737280 | tf_op jit(solution)/shard_map/reshape | solution.py:46
  257.3 9.1 %reduce_sum.412 = f32[10,18,64]{2,1,0:T(8,128)S(1)} reduce(f32[10,2,18,2,64,2]{5,4,3,2,1,0:T(8,128)} %reshape.140, f32[]{:T(128)} %constant.67.clone.1), dimensions={1,3,5}, to_apply=%region_16.17 | reduce | flops 80640 | bytes 414724 | tf_op jit(solution)/shard_map/reduce_sum | solution.py:46
  266.9 4.7 reshape.141
  293.9 4.7 collective-permute-start.18
  312.8 4.9 all-reduce.83
  321.9 11.9 %all-reduce.74 = (f32[4]{0:T(128)S(1)}, f32[4]{0:T(128)S(1)}) all-reduce(f32[4]{0:T(128)S(1)} %dynamic-update-slice.11, f32[4]{0:T(128)S(1)} %dynamic-update-slice.16), channel_id=1, replica_groups=mesh['gx_0'=2,'gx_1'=4,'gx_2'=2,'gy_0'=4,'gy_1'=2] {'gx_1'}, use_global_device_ids=true, to_apply=%add.51 | all-reduce | flops 8 | bytes 64
  344.9 9.6 %all-reduce.71 = (f32[4]{0:T(128)S(1)}, f32[4]{0:T(128)S(1)}) all-reduce(f32[4]{0:T(128)S(1)} %dynamic-update-slice.13, f32[4]{0:T(128)S(1)} %dynamic-update-slice.18), channel_id=1, replica_groups=mesh['gx_0'=2,'gx_1'=4,'gx_2'=2,'gy_0'=4,'gy_1'=2] {'gy_0'}, use_global_device_ids=true, to_apply=%add.53 | all-reduce | flops 8 | bytes 64
  358.6 6.4 %all-reduce.77 = (f32[2]{0:T(128)S(1)}, f32[2]{0:T(128)S(1)}) all-reduce(f32[2]{0:T(128)S(1)} %dynamic-update-slice.14, f32[2]{0:T(128)S(1)} %dynamic-update-slice.19), channel_id=1, replica_groups=mesh['gx_0'=2,'gx_1'=4,'gx_2'=2,'gy_0'=4,'gy_1'=2] {'gy_1'}, use_global_device_ids=true, to_apply=%add.54 | all-reduce | flops 4 | bytes 32
  381.0 5.1 collective-permute-start.23
  389.6 25.3 %reshape.148 = f32[10,2,18,2,64,2]{5,4,3,2,1,0:T(8,128)} reshape(f32[20,36,128]{2,1,0:T(8,128)S(1)} %fusion.53) | data formatting | bytes 737280 | tf_op jit(solution)/shard_map/reshape | solution.py:46
  414.8 9.1 %reduce_sum.426 = f32[10,18,64]{2,1,0:T(8,128)S(1)} reduce(f32[10,2,18,2,64,2]{5,4,3,2,1,0:T(8,128)} %reshape.148, f32[]{:T(128)} %constant.67.clone.1), dimensions={1,3,5}, to_apply=%region_30.31 | reduce | flops 80640 | bytes 414724 | tf_op jit(solution)/shard_map/reduce_sum | solution.py:46
  424.5 4.7 reshape.149
  456.9 4.7 collective-permute-start.27
  471.0 4.9 all-reduce.82
  479.9 11.9 %all-reduce.73 = (f32[4]{0:T(128)S(1)}, f32[4]{0:T(128)S(1)}) all-reduce(f32[4]{0:T(128)S(1)} %dynamic-update-slice.21, f32[4]{0:T(128)S(1)} %dynamic-update-slice.26), channel_id=1, replica_groups=mesh['gx_0'=2,'gx_1'=4,'gx_2'=2,'gy_0'=4,'gy_1'=2] {'gx_1'}, use_global_device_ids=true, to_apply=%add.61 | all-reduce | flops 8 | bytes 64
  502.4 10.6 %all-reduce.70 = (f32[4]{0:T(128)S(1)}, f32[4]{0:T(128)S(1)}) all-reduce(f32[4]{0:T(128)S(1)} %dynamic-update-slice.23, f32[4]{0:T(128)S(1)} %dynamic-update-slice.28), channel_id=1, replica_groups=mesh['gx_0'=2,'gx_1'=4,'gx_2'=2,'gy_0'=4,'gy_1'=2] {'gy_0'}, use_global_device_ids=true, to_apply=%add.63 | all-reduce | flops 8 | bytes 64
  516.9 6.4 %all-reduce.76 = (f32[2]{0:T(128)S(1)}, f32[2]{0:T(128)S(1)}) all-reduce(f32[2]{0:T(128)S(1)} %dynamic-update-slice.24, f32[2]{0:T(128)S(1)} %dynamic-update-slice.29), channel_id=1, replica_groups=mesh['gx_0'=2,'gx_1'=4,'gx_2'=2,'gy_0'=4,'gy_1'=2] {'gy_1'}, use_global_device_ids=true, to_apply=%add.64 | all-reduce | flops 4 | bytes 32
  (423 shorter events, 219.6 us)
Async XLA Ops:
  0.6 22.1 %copy-start.8 = (f32[16,32,128]{2,1,0:T(8,128)S(1)}, f32[16,32,128]{2,1,0:T(8,128)}, u32[]{:S(2)}) copy-start(f32[16,32,128]{2,1,0:T(8,128)} %param.2) | copy-start | bytes 786436
  1.5 12.0 %collective-permute-start.4 = (f32[2,32,128]{2,1,0:T(8,128)S(1)}, f32[2,32,128]{2,1,0:T(8,128)S(1)}, u32[]{:S(2)}, u32[]{:S(2)}) collective-permute-start(f32[2,32,128]{2,1,0:T(8,128)S(1)} %get-tuple-element.83), channel_id=1, source_target_pairs={{0,8},{8,16},{16,24},{24,32},{32,40},{40,48},{48,56},{56,64},{64,7... | collective-permute-start | bytes 98312 | tf_op jit(solution)/shard_map/ppermute | solution.py:23
  3.4 11.0 %collective-permute-start.5 = (f32[2,32,128]{2,1,0:T(8,128)S(1)}, f32[2,32,128]{2,1,0:T(8,128)S(1)}, u32[]{:S(2)}, u32[]{:S(2)}) collective-permute-start(f32[2,32,128]{2,1,0:T(8,128)S(1)} %get-tuple-element.82), channel_id=1, source_target_pairs={{8,0},{16,8},{24,16},{32,24},{40,32},{48,40},{56,48},{64,56},{72,6... | collective-permute-start | bytes 98312 | tf_op jit(solution)/shard_map/ppermute | solution.py:26
  7.8 14.9 %collective-permute-start = (f32[2,32,128]{2,1,0:T(8,128)S(1)}, f32[2,32,128]{2,1,0:T(8,128)S(1)}, u32[]{:S(2)}, u32[]{:S(2)}) collective-permute-start(f32[2,32,128]{2,1,0:T(8,128)S(1)} %get-tuple-element.85), channel_id=1, source_target_pairs={{0,8},{8,16},{16,24},{24,32},{32,40},{40,48},{48,56},{56,64},{64,7... | collective-permute-start | bytes 98312 | tf_op jit(solution)/shard_map/ppermute | solution.py:23
  10.0 12.8 %collective-permute-start.1 = (f32[2,32,128]{2,1,0:T(8,128)S(1)}, f32[2,32,128]{2,1,0:T(8,128)S(1)}, u32[]{:S(2)}, u32[]{:S(2)}) collective-permute-start(f32[2,32,128]{2,1,0:T(8,128)S(1)} %get-tuple-element.84), channel_id=1, source_target_pairs={{8,0},{16,8},{24,16},{32,24},{40,32},{48,40},{56,48},{64,56},{72,6... | collective-permute-start | bytes 98312 | tf_op jit(solution)/shard_map/ppermute | solution.py:26
  14.5 16.7 %collective-permute-start.6 = (f32[20,2,128]{2,1,0:T(2,128)S(1)}, f32[20,2,128]{2,1,0:T(2,128)S(1)}, u32[]{:S(2)}, u32[]{:S(2)}) collective-permute-start(f32[20,2,128]{2,1,0:T(2,128)S(1)} %get-tuple-element.74), channel_id=1, source_target_pairs={{0,1},{1,2},{2,3},{3,4},{4,5},{5,6},{6,7},{8,9},{9,10},{10,11},{11... | collective-permute-start | bytes 61448 | tf_op jit(solution)/shard_map/ppermute | solution.py:23
  18.5 12.7 %collective-permute-start.7 = (f32[20,2,128]{2,1,0:T(2,128)S(1)}, f32[20,2,128]{2,1,0:T(2,128)S(1)}, u32[]{:S(2)}, u32[]{:S(2)}) collective-permute-start(f32[20,2,128]{2,1,0:T(2,128)S(1)} %get-tuple-element.75), channel_id=1, source_target_pairs={{1,0},{2,1},{3,2},{4,3},{5,4},{6,5},{7,6},{9,8},{10,9},{11,10},{12... | collective-permute-start | bytes 61448 | tf_op jit(solution)/shard_map/ppermute | solution.py:26
  22.9 8.3 %collective-permute-start.2 = (f32[20,2,128]{2,1,0:T(2,128)S(1)}, f32[20,2,128]{2,1,0:T(2,128)S(1)}, u32[]{:S(2)}, u32[]{:S(2)}) collective-permute-start(f32[20,2,128]{2,1,0:T(2,128)S(1)} %get-tuple-element.76), channel_id=1, source_target_pairs={{0,1},{1,2},{2,3},{3,4},{4,5},{5,6},{6,7},{8,9},{9,10},{10,11},{11... | collective-permute-start | bytes 61448 | tf_op jit(solution)/shard_map/ppermute | solution.py:23
  26.0 7.2 %collective-permute-start.3 = (f32[20,2,128]{2,1,0:T(2,128)S(1)}, f32[20,2,128]{2,1,0:T(2,128)S(1)}, u32[]{:S(2)}, u32[]{:S(2)}) collective-permute-start(f32[20,2,128]{2,1,0:T(2,128)S(1)} %get-tuple-element.77), channel_id=1, source_target_pairs={{1,0},{2,1},{3,2},{4,3},{5,4},{6,5},{7,6},{9,8},{10,9},{11,10},{12... | collective-permute-start | bytes 61448 | tf_op jit(solution)/shard_map/ppermute | solution.py:26
  33.3 27.0 %copy-start = (f32[20,36,128]{2,1,0:T(8,128)}, f32[20,36,128]{2,1,0:T(8,128)S(1)}, u32[]{:S(2)}) copy-start(f32[20,36,128]{2,1,0:T(8,128)S(1)} %get-tuple-element.68) | copy-start | bytes 1105924
  125.8 6.1 %collective-permute-start.8 = (f32[2,3,38,128]{3,0,2,1:T(2,128)S(1)}, f32[2,3,38,128]{3,0,2,1:T(2,128)S(1)}, u32[]{:S(2)}, u32[]{:S(2)}) collective-permute-start(f32[2,3,38,128]{3,0,2,1:T(2,128)S(1)} %get-tuple-element.60), channel_id=1, source_target_pairs={{0,8},{8,16},{16,24},{24,32},{32,40},{40,48},{48,56},{56,64},{64,7... | collective-permute-start | bytes 350216 | tf_op jit(solution)/shard_map/ppermute | solution.py:23
  127.8 6.0 %collective-permute-start.9 = (f32[2,3,38,128]{3,0,2,1:T(2,128)S(1)}, f32[2,3,38,128]{3,0,2,1:T(2,128)S(1)}, u32[]{:S(2)}, u32[]{:S(2)}) collective-permute-start(f32[2,3,38,128]{3,0,2,1:T(2,128)S(1)} %get-tuple-element.61), channel_id=1, source_target_pairs={{8,0},{16,8},{24,16},{32,24},{40,32},{48,40},{56,48},{64,56},{72,6... | collective-permute-start | bytes 350216 | tf_op jit(solution)/shard_map/ppermute | solution.py:26
  133.9 8.9 %collective-permute-start.10 = (f32[2,28,3,128]{3,0,2,1:T(2,128)S(1)}, f32[2,28,3,128]{3,0,2,1:T(2,128)S(1)}, u32[]{:S(2)}, u32[]{:S(2)}) collective-permute-start(f32[2,28,3,128]{3,0,2,1:T(2,128)S(1)} %get-tuple-element.48), channel_id=1, source_target_pairs={{0,1},{1,2},{2,3},{3,4},{4,5},{5,6},{6,7},{8,9},{9,10},{10,11},{11... | collective-permute-start | bytes 258056 | tf_op jit(solution)/shard_map/ppermute | solution.py:23
  140.1 7.9 %collective-permute-start.11 = (f32[2,28,3,128]{3,0,2,1:T(2,128)S(1)}, f32[2,28,3,128]{3,0,2,1:T(2,128)S(1)}, u32[]{:S(2)}, u32[]{:S(2)}) collective-permute-start(f32[2,28,3,128]{3,0,2,1:T(2,128)S(1)} %get-tuple-element.49), channel_id=1, source_target_pairs={{1,0},{2,1},{3,2},{4,3},{5,4},{6,5},{7,6},{9,8},{10,9},{11,10},{12... | collective-permute-start | bytes 258056 | tf_op jit(solution)/shard_map/ppermute | solution.py:26
  150.7 33.2 %copy-start.13 = (u32[128]{0:T(128)S(1)}, u32[128]{0:T(128)}, u32[]{:S(2)}) copy-start(u32[128]{0:T(128)} %constant.182) | copy-start | bytes 1540
  150.7 40.3 %copy-start.12 = (u32[128]{0:T(128)S(1)}, u32[128]{0:T(128)}, u32[]{:S(2)}) copy-start(u32[128]{0:T(128)} %constant.187) | copy-start | bytes 1540
  213.1 5.6 %collective-permute-start.12 = (f32[2,32,128]{2,1,0:T(8,128)S(1)}, f32[2,32,128]{2,1,0:T(8,128)S(1)}, u32[]{:S(2)}, u32[]{:S(2)}) collective-permute-start(f32[2,32,128]{2,1,0:T(8,128)S(1)} %get-tuple-element.80), channel_id=1, source_target_pairs={{0,8},{8,16},{16,24},{24,32},{32,40},{40,48},{48,56},{56,64},{64,7... | collective-permute-start | bytes 98312 | tf_op jit(solution)/shard_map/ppermute | solution.py:23
  215.1 5.2 collective-permute-start.13
  220.3 8.7 %collective-permute-start.14 = (f32[20,2,128]{2,1,0:T(2,128)S(1)}, f32[20,2,128]{2,1,0:T(2,128)S(1)}, u32[]{:S(2)}, u32[]{:S(2)}) collective-permute-start(f32[20,2,128]{2,1,0:T(2,128)S(1)} %get-tuple-element.72), channel_id=1, source_target_pairs={{0,1},{1,2},{2,3},{3,4},{4,5},{5,6},{6,7},{8,9},{9,10},{10,11},{11... | collective-permute-start | bytes 61448 | tf_op jit(solution)/shard_map/ppermute | solution.py:23
  223.4 7.2 %collective-permute-start.15 = (f32[20,2,128]{2,1,0:T(2,128)S(1)}, f32[20,2,128]{2,1,0:T(2,128)S(1)}, u32[]{:S(2)}, u32[]{:S(2)}) collective-permute-start(f32[20,2,128]{2,1,0:T(2,128)S(1)} %get-tuple-element.73), channel_id=1, source_target_pairs={{1,0},{2,1},{3,2},{4,3},{5,4},{6,5},{7,6},{9,8},{10,9},{11,10},{12... | collective-permute-start | bytes 61448 | tf_op jit(solution)/shard_map/ppermute | solution.py:26
  285.8 6.1 %collective-permute-start.16 = (f32[2,3,38,128]{3,0,2,1:T(2,128)S(1)}, f32[2,3,38,128]{3,0,2,1:T(2,128)S(1)}, u32[]{:S(2)}, u32[]{:S(2)}) collective-permute-start(f32[2,3,38,128]{3,0,2,1:T(2,128)S(1)} %get-tuple-element.58), channel_id=1, source_target_pairs={{0,8},{8,16},{16,24},{24,32},{32,40},{40,48},{48,56},{56,64},{64,7... | collective-permute-start | bytes 350216 | tf_op jit(solution)/shard_map/ppermute | solution.py:23
  287.7 6.0 %collective-permute-start.17 = (f32[2,3,38,128]{3,0,2,1:T(2,128)S(1)}, f32[2,3,38,128]{3,0,2,1:T(2,128)S(1)}, u32[]{:S(2)}, u32[]{:S(2)}) collective-permute-start(f32[2,3,38,128]{3,0,2,1:T(2,128)S(1)} %get-tuple-element.59), channel_id=1, source_target_pairs={{8,0},{16,8},{24,16},{32,24},{40,32},{48,40},{56,48},{64,56},{72,6... | collective-permute-start | bytes 350216 | tf_op jit(solution)/shard_map/ppermute | solution.py:26
  293.9 8.8 %collective-permute-start.18 = (f32[2,28,3,128]{3,0,2,1:T(2,128)S(1)}, f32[2,28,3,128]{3,0,2,1:T(2,128)S(1)}, u32[]{:S(2)}, u32[]{:S(2)}) collective-permute-start(f32[2,28,3,128]{3,0,2,1:T(2,128)S(1)} %get-tuple-element.46), channel_id=1, source_target_pairs={{0,1},{1,2},{2,3},{3,4},{4,5},{5,6},{6,7},{8,9},{9,10},{10,11},{11... | collective-permute-start | bytes 258056 | tf_op jit(solution)/shard_map/ppermute | solution.py:23
  298.6 7.9 %collective-permute-start.19 = (f32[2,28,3,128]{3,0,2,1:T(2,128)S(1)}, f32[2,28,3,128]{3,0,2,1:T(2,128)S(1)}, u32[]{:S(2)}, u32[]{:S(2)}) collective-permute-start(f32[2,28,3,128]{3,0,2,1:T(2,128)S(1)} %get-tuple-element.47), channel_id=1, source_target_pairs={{1,0},{2,1},{3,2},{4,3},{5,4},{6,5},{7,6},{9,8},{10,9},{11,10},{12... | collective-permute-start | bytes 258056 | tf_op jit(solution)/shard_map/ppermute | solution.py:26
  370.7 5.6 %collective-permute-start.20 = (f32[2,32,128]{2,1,0:T(8,128)S(1)}, f32[2,32,128]{2,1,0:T(8,128)S(1)}, u32[]{:S(2)}, u32[]{:S(2)}) collective-permute-start(f32[2,32,128]{2,1,0:T(8,128)S(1)} %get-tuple-element.78), channel_id=1, source_target_pairs={{0,8},{8,16},{16,24},{24,32},{32,40},{40,48},{48,56},{56,64},{64,7... | collective-permute-start | bytes 98312 | tf_op jit(solution)/shard_map/ppermute | solution.py:23
  372.6 5.2 collective-permute-start.21
  377.9 8.3 %collective-permute-start.22 = (f32[20,2,128]{2,1,0:T(2,128)S(1)}, f32[20,2,128]{2,1,0:T(2,128)S(1)}, u32[]{:S(2)}, u32[]{:S(2)}) collective-permute-start(f32[20,2,128]{2,1,0:T(2,128)S(1)} %get-tuple-element.70), channel_id=1, source_target_pairs={{0,1},{1,2},{2,3},{3,4},{4,5},{5,6},{6,7},{8,9},{9,10},{10,11},{11... | collective-permute-start | bytes 61448 | tf_op jit(solution)/shard_map/ppermute | solution.py:23
  381.0 7.2 %collective-permute-start.23 = (f32[20,2,128]{2,1,0:T(2,128)S(1)}, f32[20,2,128]{2,1,0:T(2,128)S(1)}, u32[]{:S(2)}, u32[]{:S(2)}) collective-permute-start(f32[20,2,128]{2,1,0:T(2,128)S(1)} %get-tuple-element.71), channel_id=1, source_target_pairs={{1,0},{2,1},{3,2},{4,3},{5,4},{6,5},{7,6},{9,8},{10,9},{11,10},{12... | collective-permute-start | bytes 61448 | tf_op jit(solution)/shard_map/ppermute | solution.py:26
  445.1 6.1 %collective-permute-start.24 = (f32[2,3,38,128]{3,0,2,1:T(2,128)S(1)}, f32[2,3,38,128]{3,0,2,1:T(2,128)S(1)}, u32[]{:S(2)}, u32[]{:S(2)}) collective-permute-start(f32[2,3,38,128]{3,0,2,1:T(2,128)S(1)} %get-tuple-element.56), channel_id=1, source_target_pairs={{0,8},{8,16},{16,24},{24,32},{32,40},{40,48},{48,56},{56,64},{64,7... | collective-permute-start | bytes 350216 | tf_op jit(solution)/shard_map/ppermute | solution.py:23
  447.0 6.0 %collective-permute-start.25 = (f32[2,3,38,128]{3,0,2,1:T(2,128)S(1)}, f32[2,3,38,128]{3,0,2,1:T(2,128)S(1)}, u32[]{:S(2)}, u32[]{:S(2)}) collective-permute-start(f32[2,3,38,128]{3,0,2,1:T(2,128)S(1)} %get-tuple-element.57), channel_id=1, source_target_pairs={{8,0},{16,8},{24,16},{32,24},{40,32},{48,40},{56,48},{64,56},{72,6... | collective-permute-start | bytes 350216 | tf_op jit(solution)/shard_map/ppermute | solution.py:26
  453.2 8.8 %collective-permute-start.26 = (f32[2,28,3,128]{3,0,2,1:T(2,128)S(1)}, f32[2,28,3,128]{3,0,2,1:T(2,128)S(1)}, u32[]{:S(2)}, u32[]{:S(2)}) collective-permute-start(f32[2,28,3,128]{3,0,2,1:T(2,128)S(1)} %get-tuple-element.44), channel_id=1, source_target_pairs={{0,1},{1,2},{2,3},{3,4},{4,5},{5,6},{6,7},{8,9},{9,10},{10,11},{11... | collective-permute-start | bytes 258056 | tf_op jit(solution)/shard_map/ppermute | solution.py:23
  456.9 7.9 %collective-permute-start.27 = (f32[2,28,3,128]{3,0,2,1:T(2,128)S(1)}, f32[2,28,3,128]{3,0,2,1:T(2,128)S(1)}, u32[]{:S(2)}, u32[]{:S(2)}) collective-permute-start(f32[2,28,3,128]{3,0,2,1:T(2,128)S(1)} %get-tuple-element.45), channel_id=1, source_target_pairs={{1,0},{2,1},{3,2},{4,3},{5,4},{6,5},{7,6},{9,8},{10,9},{11,10},{12... | collective-permute-start | bytes 258056 | tf_op jit(solution)/shard_map/ppermute | solution.py:26
  (13 other events, 63.5 us)
